TPU v7x, 32 devices: a whole 2x2x4 slice. The times are simulated.
32 devices in a mesh: agents: 8 (over z, x), group: 4 (over y, core).
Axes of the slice: x: 2, y: 2, z: 4, core: 2. Of those that a mesh axis runs over, the one named last changes fastest.
Arguments:
- q_lin: float32 [4, 40, 2048], P('group', None, 'agents'), may hold values from -6 to 6
- inverse: bfloat16 [4, 40, 40, 2048], P('group', None, None, 'agents'), may hold values from -0.5 to 1, as said below
- predict: bfloat16 [4, 40, 40, 2048], P('group', None, None, 'agents'), may hold values from -1 to 1
- free_traj: float32 [4, 40, 2048], P('group', None, 'agents'), may hold values from -6 to 6
- offsets: float32 [4, 8, 40, 2048], P('group', None, None, 'agents'), may hold values from -4 to 4
- multipliers: float32 [4, 8, 40, 2048], P('group', None, None, 'agents'), may hold values from -4 to 4
- nbr_owner: int32 [4, 8, 2048], P('group', None, 'agents'), may hold values from 0 to 7, as said below
- nbr_slot: int32 [4, 8, 2048], P('group', None, 'agents'), may hold values from -1 to 255
- platoon: int32 [4, 2048], P('group', 'agents'), may hold values from 0 to 127, as said below
Outputs:
- inputs_plan: float32 [4, 40, 2048], P('group', None, 'agents')
- multipliers_out: float32 [4, 8, 40, 2048], P('group', None, None, 'agents')
Inputs may be any that keep to these rules, and one draw needn't show every extreme that they name: `nbr_owner`: an agent's own block index is its row in the region // 256; each neighbour's owner lies within 2 blocks of it, slot 0 is never padded. `inverse`: symmetric for every agent. `platoon`: 32 or more platoons hold no agent of any region.
All inputs are finite; a program needn't handle non-finite values. Where the computation divides by a largest or mean magnitude, that divisor is 1e-20 or more.
Results may differ from a plain program's by a relative error of at most 0.0003.
Values sent between devices are 32-bit elements; how exact they have to be, the bound alone decides.
A program may use at most 64 MiB of HBM per device.

v0:
```python
import jax
import jax.numpy as jnp
from jax import lax
from jax.sharding import PartitionSpec as P

SPAN = 2
NPLAT = 128
ITERS = 3


RHO = 0.5
KAPPA = 0.5


def shifted(value, axis, steps):
    count = lax.axis_size(axis)
    first, last = (max(0, -steps), min(count, count - steps))
    return lax.ppermute(value, axis, [(source, source + steps) for source in range(first, last)])


def local(q_lin, inverse, predict, free_traj, offsets, multipliers, nbr_owner, nbr_slot, platoon):
    block = q_lin.shape[2]
    traj_len = free_traj.shape[1]
    alive = nbr_slot >= 0
    live = alive.astype(jnp.float32)[:, :, None, :]
    onehot = (platoon[:, None, :] == jnp.arange(NPLAT, dtype=jnp.int32)[None, :, None]).astype(
        jnp.float32
    )
    counts_local = jnp.sum(onehot, axis=(0, 2))
    mine = lax.axis_index("agents")
    column = (nbr_owner - mine + SPAN) * block + nbr_slot
    column = jnp.where(alive, column, 0)[0].reshape(-1)

    def lookup(field):
        pieces = []
        for distance in range(-SPAN, SPAN + 1):
            if distance == 0:
                pieces.append(field)
            else:
                pieces.append(shifted(field, "agents", -distance))
        joined = jnp.concatenate(pieces, axis=2)
        taken = jnp.take(joined[0], column, axis=1).reshape(traj_len, nbr_slot.shape[1], block)
        return jnp.transpose(taken, (1, 0, 2))[None] * live

    def platoon_local(field):
        return jnp.einsum("rta,rpa->tp", field, onehot, precision=lax.Precision.HIGHEST)

    traj = free_traj
    lam = multipliers
    near = lookup(traj)
    sums, counts = lax.psum((platoon_local(traj), counts_local), ("agents", "group"))
    divisor = jnp.maximum(counts, 1.0)[None, :]

    def spread(totals):
        means = totals / divisor
        return jnp.einsum("tp,rpa->rta", means, onehot, precision=lax.Precision.HIGHEST)

    attract = spread(sums)
    plan = jnp.zeros_like(q_lin)
    for step in range(ITERS):
        coupling = jnp.sum(live * (lam - RHO * (near + offsets)), axis=1) - KAPPA * attract
        rhs = q_lin + jnp.einsum(
            "rtja,rta->rja", predict.astype(jnp.float32), coupling, precision=lax.Precision.HIGHEST
        )
        plan = -jnp.einsum(
            "rija,rja->ria", inverse.astype(jnp.float32), rhs, precision=lax.Precision.HIGHEST
        )
        traj = (
            jnp.einsum(
                "rtja,rja->rta", predict.astype(jnp.float32), plan, precision=lax.Precision.HIGHEST
            )
            + free_traj
        )
        near = lookup(traj)
        gap = live * (traj[:, None] - near - offsets)
        local_peak = jnp.max(jnp.abs(gap))
        more = step + 1 < ITERS
        peak = lax.pmax(local_peak, ("agents", "group"))
        if more:
            sums = lax.psum(platoon_local(traj), ("agents", "group"))
        lam = lam + gap / (1.0 + peak)
        if more:
            attract = spread(sums)
    return (plan, lam)


def solution(mesh):
    return jax.shard_map(
        local,
        mesh=mesh,
        in_specs=(
            P("group", None, "agents"),
            P("group", None, None, "agents"),
            P("group", None, None, "agents"),
            P("group", None, "agents"),
            P("group", None, None, "agents"),
            P("group", None, None, "agents"),
            P("group", None, "agents"),
            P("group", None, "agents"),
            P("group", "agents"),
        ),
        out_specs=(P("group", None, "agents"), P("group", None, None, "agents")),
        check_vma=False,
    )
```

profile of v0, /device:TPU:0, one launch (start us, length us, event | category | flops | bytes accessed | tf_op | source)
XLA Modules:
  0.0 352.8 jit_solution(9118667812695265444)
XLA Ops:
  0.6 5.0 %collective-permute-start = (f32[1,40,256]{2,1,0:T(8,128)}, f32[1,40,256]{2,1,0:T(8,128)S(1)}, u32[]{:S(2)}, u32[]{:S(2)}) collective-permute-start(f32[1,40,256]{2,1,0:T(8,128)} %param.14), channel_id=1, source_target_pairs={{0,8},{4,12},{8,16},{12,20},{16,24},{20,28},{1,9},{5,13},{9,17},{1... | collective-permute-start | bytes 122888 | tf_op jit(solution)/shard_map/ppermute | solution.py:18
  5.6 3.4 collective-permute-start.1
  14.9 42.9 %all-reduce = (f32[40,128]{1,0:T(8,128)S(1)}, f32[128]{0:T(128)S(1)}) all-reduce(f32[40,128]{1,0:T(8,128)S(1)} %convolution_bitcast_fusion, f32[128]{0:T(128)S(1)} %convert_reduce_fusion), channel_id=1, replica_groups=mesh['agents'=8,'group'=4] {'agents','group'}, use_global_device_ids=true, to_apply=%region_1.3 | all-reduce | flops 5248 | bytes 41984 | tf_op jit(solution)/shard_map/psum | solution.py:51
  58.9 5.5 %gather_fusion = f32[2048,40]{1,0:T(8,128)S(1)} fusion(f32[40,1280]{0,1:T(8,128)S(1)} %bitcast.254, s32[2048]{0:T(1024)S(1)} %fusion.51), kind=kCustom, calls=%fused_computation.clone | custom fusion | bytes 663552 | tf_op jit(solution)/shard_map/jit(_take)/gather | solution.py:42
  68.2 3.4 collective-permute-start.4
  71.6 4.2 %collective-permute-start.5 = (f32[1,40,256]{2,1,0:T(8,128)S(1)}, f32[1,40,256]{2,1,0:T(8,128)S(1)}, u32[]{:S(2)}, u32[]{:S(2)}) collective-permute-start(f32[1,40,256]{2,1,0:T(8,128)S(1)} %bitcast_add_fusion.7), channel_id=1, source_target_pairs={{0,4},{4,8},{8,12},{12,16},{16,20},{20,24},{24,28},{1,5},{5,9},{9,... | collective-permute-start | bytes 122888 | tf_op jit(solution)/shard_map/ppermute | solution.py:18
  78.7 3.0 collective-permute-done.6
  81.7 1.9 collective-permute-done.7
  83.9 7.6 %gather_fusion.1 = f32[2048,40]{1,0:T(8,128)} fusion(f32[40,1280]{0,1:T(8,128)S(1)} %bitcast.255, s32[2048]{0:T(1024)S(1)} %fusion.51), kind=kCustom, calls=%fused_computation.1.clone | custom fusion | bytes 663552 | tf_op jit(solution)/shard_map/jit(_take)/gather | solution.py:42
  94.0 40.7 %psum.30 = f32[40,128]{1,0:T(8,128)S(1)} all-reduce(f32[40,128]{1,0:T(8,128)S(1)} %fusion.34), channel_id=1, replica_groups=mesh['agents'=8,'group'=4] {'agents','group'}, use_global_device_ids=true, to_apply=%region_7.9 | all-reduce | flops 5120 | bytes 40960 | tf_op jit(solution)/shard_map/psum | solution.py:80
  134.7 39.7 %pmax.21 = f32[]{:T(128)} all-reduce(f32[]{:T(128)} %abs_reduce_fusion.2), channel_id=1, replica_groups=mesh['agents'=8,'group'=4] {'agents','group'}, use_global_device_ids=true, to_apply=%region_5.7 | all-reduce | flops 1 | bytes 8 | tf_op jit(solution)/shard_map/pmax | solution.py:78
  177.2 4.0 %collective-permute-start.8 = (f32[1,40,256]{2,1,0:T(8,128)S(1)}, f32[1,40,256]{2,1,0:T(8,128)S(1)}, u32[]{:S(2)}, u32[]{:S(2)}) collective-permute-start(f32[1,40,256]{2,1,0:T(8,128)S(1)} %bitcast_add_fusion.5), channel_id=1, source_target_pairs={{0,8},{4,12},{8,16},{12,20},{16,24},{20,28},{1,9},{5,13},{9,17},{1... | collective-permute-start | bytes 122888 | tf_op jit(solution)/shard_map/ppermute | solution.py:18
  181.3 4.2 %collective-permute-start.9 = (f32[1,40,256]{2,1,0:T(8,128)S(1)}, f32[1,40,256]{2,1,0:T(8,128)S(1)}, u32[]{:S(2)}, u32[]{:S(2)}) collective-permute-start(f32[1,40,256]{2,1,0:T(8,128)S(1)} %bitcast_add_fusion.5), channel_id=1, source_target_pairs={{0,4},{4,8},{8,12},{12,16},{16,20},{20,24},{24,28},{1,5},{5,9},{9,... | collective-permute-start | bytes 122888 | tf_op jit(solution)/shard_map/ppermute | solution.py:18
  188.4 3.0 collective-permute-done.10
  193.0 7.6 %gather_fusion.2 = f32[2048,40]{1,0:T(8,128)} fusion(f32[40,1280]{0,1:T(8,128)S(1)} %bitcast.256, s32[2048]{0:T(1024)S(1)} %fusion.51), kind=kCustom, calls=%fused_computation.2.clone | custom fusion | bytes 663552 | tf_op jit(solution)/shard_map/jit(_take)/gather | solution.py:42
  200.6 1.6 broadcast_select_fusion.1
  203.2 1.6 abs_reduce_fusion.1
  204.8 40.1 %psum.31 = f32[40,128]{1,0:T(8,128)S(1)} all-reduce(f32[40,128]{1,0:T(8,128)S(1)} %fusion.33), channel_id=1, replica_groups=mesh['agents'=8,'group'=4] {'agents','group'}, use_global_device_ids=true, to_apply=%region_11.13 | all-reduce | flops 5120 | bytes 40960 | tf_op jit(solution)/shard_map/psum | solution.py:80
  244.9 40.5 %pmax.22 = f32[]{:T(128)} all-reduce(f32[]{:T(128)} %abs_reduce_fusion.1), channel_id=1, replica_groups=mesh['agents'=8,'group'=4] {'agents','group'}, use_global_device_ids=true, to_apply=%region_9.11 | all-reduce | flops 1 | bytes 8 | tf_op jit(solution)/shard_map/pmax | solution.py:78
  288.9 3.6 %collective-permute-start.12 = (f32[1,40,256]{2,1,0:T(8,128)S(1)}, f32[1,40,256]{2,1,0:T(8,128)S(1)}, u32[]{:S(2)}, u32[]{:S(2)}) collective-permute-start(f32[1,40,256]{2,1,0:T(8,128)S(1)} %bitcast_add_fusion.3), channel_id=1, source_target_pairs={{0,8},{4,12},{8,16},{12,20},{16,24},{20,28},{1,9},{5,13},{9,17},{1... | collective-permute-start | bytes 122888 | tf_op jit(solution)/shard_map/ppermute | solution.py:18
  292.5 4.2 %collective-permute-start.13 = (f32[1,40,256]{2,1,0:T(8,128)S(1)}, f32[1,40,256]{2,1,0:T(8,128)S(1)}, u32[]{:S(2)}, u32[]{:S(2)}) collective-permute-start(f32[1,40,256]{2,1,0:T(8,128)S(1)} %bitcast_add_fusion.3), channel_id=1, source_target_pairs={{0,4},{4,8},{8,12},{12,16},{16,20},{20,24},{24,28},{1,5},{5,9},{9,... | collective-permute-start | bytes 122888 | tf_op jit(solution)/shard_map/ppermute | solution.py:18
  299.4 3.2 collective-permute-done.14
  304.2 5.5 %gather_fusion.3 = f32[2048,40]{1,0:T(8,128)S(1)} fusion(f32[40,1280]{0,1:T(8,128)S(1)} %bitcast.253, s32[2048]{0:T(1024)S(1)} %fusion.51), kind=kCustom, calls=%fused_computation.3.clone | custom fusion | bytes 663552 | tf_op jit(solution)/shard_map/jit(_take)/gather | solution.py:42
  311.0 40.3 %pmax.23 = f32[]{:T(128)} all-reduce(f32[]{:T(128)} %abs_reduce_fusion), channel_id=1, replica_groups=mesh['agents'=8,'group'=4] {'agents','group'}, use_global_device_ids=true, to_apply=%region_13.15 | all-reduce | flops 1 | bytes 8 | tf_op jit(solution)/shard_map/pmax | solution.py:78
  (106 shorter events, 32.9 us)
Async XLA Ops:
  0.6 57.2 %collective-permute-start = (f32[1,40,256]{2,1,0:T(8,128)}, f32[1,40,256]{2,1,0:T(8,128)S(1)}, u32[]{:S(2)}, u32[]{:S(2)}) collective-permute-start(f32[1,40,256]{2,1,0:T(8,128)} %param.14), channel_id=1, source_target_pairs={{0,8},{4,12},{8,16},{12,20},{16,24},{20,28},{1,9},{5,13},{9,17},{1... | collective-permute-start | bytes 122888 | tf_op jit(solution)/shard_map/ppermute | solution.py:18
  5.6 52.2 %collective-permute-start.1 = (f32[1,40,256]{2,1,0:T(8,128)}, f32[1,40,256]{2,1,0:T(8,128)S(1)}, u32[]{:S(2)}, u32[]{:S(2)}) collective-permute-start(f32[1,40,256]{2,1,0:T(8,128)} %param.14), channel_id=1, source_target_pairs={{0,4},{4,8},{8,12},{12,16},{16,20},{20,24},{24,28},{1,5},{5,9},{9,... | collective-permute-start | bytes 122888 | tf_op jit(solution)/shard_map/ppermute | solution.py:18
  9.0 49.6 %collective-permute-start.2 = (f32[1,40,256]{2,1,0:T(8,128)}, f32[1,40,256]{2,1,0:T(8,128)S(1)}, u32[]{:S(2)}, u32[]{:S(2)}) collective-permute-start(f32[1,40,256]{2,1,0:T(8,128)} %param.14), channel_id=1, source_target_pairs={{4,0},{8,4},{12,8},{16,12},{20,16},{24,20},{28,24},{5,1},{9,5},{13... | collective-permute-start | bytes 122888 | tf_op jit(solution)/shard_map/ppermute | solution.py:18
  10.3 48.3 %collective-permute-start.3 = (f32[1,40,256]{2,1,0:T(8,128)}, f32[1,40,256]{2,1,0:T(8,128)S(1)}, u32[]{:S(2)}, u32[]{:S(2)}) collective-permute-start(f32[1,40,256]{2,1,0:T(8,128)} %param.14), channel_id=1, source_target_pairs={{8,0},{12,4},{16,8},{20,12},{24,16},{28,20},{9,1},{13,5},{17,9},{2... | collective-permute-start | bytes 122888 | tf_op jit(solution)/shard_map/ppermute | solution.py:18
  64.7 1.1 copy-start.1
  64.7 1.1 copy-start.3
  64.8 2.2 copy-start.6
  64.8 2.4 copy-start
  65.8 1.6 copy-start.5
  65.8 1.6 copy-start.2
  67.5 0.8 copy-start.4
  68.2 10.4 %collective-permute-start.4 = (f32[1,40,256]{2,1,0:T(8,128)S(1)}, f32[1,40,256]{2,1,0:T(8,128)S(1)}, u32[]{:S(2)}, u32[]{:S(2)}) collective-permute-start(f32[1,40,256]{2,1,0:T(8,128)S(1)} %bitcast_add_fusion.7), channel_id=1, source_target_pairs={{0,8},{4,12},{8,16},{12,20},{16,24},{20,28},{1,9},{5,13},{9,17},{1... | collective-permute-start | bytes 122888 | tf_op jit(solution)/shard_map/ppermute | solution.py:18
  71.6 7.0 %collective-permute-start.5 = (f32[1,40,256]{2,1,0:T(8,128)S(1)}, f32[1,40,256]{2,1,0:T(8,128)S(1)}, u32[]{:S(2)}, u32[]{:S(2)}) collective-permute-start(f32[1,40,256]{2,1,0:T(8,128)S(1)} %bitcast_add_fusion.7), channel_id=1, source_target_pairs={{0,4},{4,8},{8,12},{12,16},{16,20},{20,24},{24,28},{1,5},{5,9},{9,... | collective-permute-start | bytes 122888 | tf_op jit(solution)/shard_map/ppermute | solution.py:18
  75.8 5.9 %collective-permute-start.6 = (f32[1,40,256]{2,1,0:T(8,128)S(1)}, f32[1,40,256]{2,1,0:T(8,128)S(1)}, u32[]{:S(2)}, u32[]{:S(2)}) collective-permute-start(f32[1,40,256]{2,1,0:T(8,128)S(1)} %bitcast_add_fusion.7), channel_id=1, source_target_pairs={{4,0},{8,4},{12,8},{16,12},{20,16},{24,20},{28,24},{5,1},{9,5},{13... | collective-permute-start | bytes 122888 | tf_op jit(solution)/shard_map/ppermute | solution.py:18
  77.1 6.5 %collective-permute-start.7 = (f32[1,40,256]{2,1,0:T(8,128)S(1)}, f32[1,40,256]{2,1,0:T(8,128)S(1)}, u32[]{:S(2)}, u32[]{:S(2)}) collective-permute-start(f32[1,40,256]{2,1,0:T(8,128)S(1)} %bitcast_add_fusion.7), channel_id=1, source_target_pairs={{8,0},{12,4},{16,8},{20,12},{24,16},{28,20},{9,1},{13,5},{17,9},{2... | collective-permute-start | bytes 122888 | tf_op jit(solution)/shard_map/ppermute | solution.py:18
  177.2 11.1 %collective-permute-start.8 = (f32[1,40,256]{2,1,0:T(8,128)S(1)}, f32[1,40,256]{2,1,0:T(8,128)S(1)}, u32[]{:S(2)}, u32[]{:S(2)}) collective-permute-start(f32[1,40,256]{2,1,0:T(8,128)S(1)} %bitcast_add_fusion.5), channel_id=1, source_target_pairs={{0,8},{4,12},{8,16},{12,20},{16,24},{20,28},{1,9},{5,13},{9,17},{1... | collective-permute-start | bytes 122888 | tf_op jit(solution)/shard_map/ppermute | solution.py:18
  181.3 7.0 %collective-permute-start.9 = (f32[1,40,256]{2,1,0:T(8,128)S(1)}, f32[1,40,256]{2,1,0:T(8,128)S(1)}, u32[]{:S(2)}, u32[]{:S(2)}) collective-permute-start(f32[1,40,256]{2,1,0:T(8,128)S(1)} %bitcast_add_fusion.5), channel_id=1, source_target_pairs={{0,4},{4,8},{8,12},{12,16},{16,20},{20,24},{24,28},{1,5},{5,9},{9,... | collective-permute-start | bytes 122888 | tf_op jit(solution)/shard_map/ppermute | solution.py:18
  185.5 5.9 %collective-permute-start.10 = (f32[1,40,256]{2,1,0:T(8,128)S(1)}, f32[1,40,256]{2,1,0:T(8,128)S(1)}, u32[]{:S(2)}, u32[]{:S(2)}) collective-permute-start(f32[1,40,256]{2,1,0:T(8,128)S(1)} %bitcast_add_fusion.5), channel_id=1, source_target_pairs={{4,0},{8,4},{12,8},{16,12},{20,16},{24,20},{28,24},{5,1},{9,5},{13... | collective-permute-start | bytes 122888 | tf_op jit(solution)/shard_map/ppermute | solution.py:18
  186.8 6.0 %collective-permute-start.11 = (f32[1,40,256]{2,1,0:T(8,128)S(1)}, f32[1,40,256]{2,1,0:T(8,128)S(1)}, u32[]{:S(2)}, u32[]{:S(2)}) collective-permute-start(f32[1,40,256]{2,1,0:T(8,128)S(1)} %bitcast_add_fusion.5), channel_id=1, source_target_pairs={{8,0},{12,4},{16,8},{20,12},{24,16},{28,20},{9,1},{13,5},{17,9},{2... | collective-permute-start | bytes 122888 | tf_op jit(solution)/shard_map/ppermute | solution.py:18
  288.9 10.5 %collective-permute-start.12 = (f32[1,40,256]{2,1,0:T(8,128)S(1)}, f32[1,40,256]{2,1,0:T(8,128)S(1)}, u32[]{:S(2)}, u32[]{:S(2)}) collective-permute-start(f32[1,40,256]{2,1,0:T(8,128)S(1)} %bitcast_add_fusion.3), channel_id=1, source_target_pairs={{0,8},{4,12},{8,16},{12,20},{16,24},{20,28},{1,9},{5,13},{9,17},{1... | collective-permute-start | bytes 122888 | tf_op jit(solution)/shard_map/ppermute | solution.py:18
  292.5 6.8 %collective-permute-start.13 = (f32[1,40,256]{2,1,0:T(8,128)S(1)}, f32[1,40,256]{2,1,0:T(8,128)S(1)}, u32[]{:S(2)}, u32[]{:S(2)}) collective-permute-start(f32[1,40,256]{2,1,0:T(8,128)S(1)} %bitcast_add_fusion.3), channel_id=1, source_target_pairs={{0,4},{4,8},{8,12},{12,16},{16,20},{20,24},{24,28},{1,5},{5,9},{9,... | collective-permute-start | bytes 122888 | tf_op jit(solution)/shard_map/ppermute | solution.py:18
  296.7 5.9 %collective-permute-start.14 = (f32[1,40,256]{2,1,0:T(8,128)S(1)}, f32[1,40,256]{2,1,0:T(8,128)S(1)}, u32[]{:S(2)}, u32[]{:S(2)}) collective-permute-start(f32[1,40,256]{2,1,0:T(8,128)S(1)} %bitcast_add_fusion.3), channel_id=1, source_target_pairs={{4,0},{8,4},{12,8},{16,12},{20,16},{24,20},{28,24},{5,1},{9,5},{13... | collective-permute-start | bytes 122888 | tf_op jit(solution)/shard_map/ppermute | solution.py:18
  298.0 6.0 %collective-permute-start.15 = (f32[1,40,256]{2,1,0:T(8,128)S(1)}, f32[1,40,256]{2,1,0:T(8,128)S(1)}, u32[]{:S(2)}, u32[]{:S(2)}) collective-permute-start(f32[1,40,256]{2,1,0:T(8,128)S(1)} %bitcast_add_fusion.3), channel_id=1, source_target_pairs={{8,0},{12,4},{16,8},{20,12},{24,16},{28,20},{9,1},{13,5},{17,9},{2... | collective-permute-start | bytes 122888 | tf_op jit(solution)/shard_map/ppermute | solution.py:18
where the time goes:
time: 355 us; the launch traced here: 353 us
  blocking collectives  244 us (69%)
  starting transfers between devices  42.3 us (12%)
  local copies, waits for them, and re-layouts  31.1 us (9%)
  other arithmetic  16.1 us (5%)
  waiting for transfers between devices  14 us (4%)
    pmax x3, blocking collectives, local(): peak = lax.pmax(local_peak, ('agents', 'group'))  120 us
    psum x2, blocking collectives, local(): sums = lax.psum(platoon_local(traj), ('agents', 'group'))  80.8 us
    psum x1, blocking collectives, local(): lax.psum((platoon_local(traj), counts_local), ('agents', 'group'))  42.9 us
    ppermute x16, starting transfers between devices, shifted(): lax.ppermute(value, axis, [(source, source + steps) for source in range(f...  42.3 us
    gather x4, local copies, waits for them, and re-layouts, lookup(): jnp.take(joined[0], column, axis=1)  26.1 us
    ppermute x16, waiting for transfers between devices, shifted(): lax.ppermute(value, axis, [(source, source + steps) for source in range(f...  14 us
  transfers between devices with their start and end apart: 16, of which 6 were waited for; matrix products, arithmetic and copies ran while one was open for 1% of the time, Pallas kernels for 0%

commit v1 on v0

v1 whole, which is shorter than its diff:
```python
import functools

import jax
import jax.numpy as jnp
from jax import lax
from jax.experimental import pallas as pl
from jax.experimental.pallas import tpu as pltpu
from jax.sharding import PartitionSpec as P

SPAN = 2
NPLAT = 128
ITERS = 3
RHO = 0.5
KAPPA = 0.5
LANES = 128
F32 = jnp.float32
BF16 = jnp.bfloat16
MESH = pl.DeviceIdType.MESH


def split(value):
    high = value.astype(BF16)
    low = (value - high.astype(F32)).astype(BF16)
    return high, low


def kernel(
    agents, group, fold,
    q_hbm, inv_hbm, pre_hbm, free_hbm, off_hbm, mul_hbm, owner_hbm, slot_hbm, plat_hbm,
    plan_hbm, lam_hbm,
    q, inv, pre, off, lam, owner, slot, plat,
    plan, gap, coup, rhs, traj, near_in,
    rs_out, rs_in, line_out, line_in, ag_out, ag_in, peak_out, peak_in, top_out, top_in,
    inv_count, lane_tab, tile_tab,
    load_sem, store_sem,
    near_send, near_recv, rs_send, rs_recv, line_send, line_recv, ag_send, ag_recv,
    peak_send, peak_recv, top_send, top_recv,
):
    me = lax.axis_index("agents")
    mine = lax.axis_index("group")
    lines = agents // fold
    plane = fold * group
    high, low = me // fold, me % fold
    spot = low * group + mine
    rows, block = q.shape
    degree = slot.shape[0]
    halves = block // LANES
    part = -(-rows // plane)

    loads = {}
    for number, (name, source, target) in enumerate((
        ("free", free_hbm, traj.at[0]), ("plat", plat_hbm, plat), ("slot", slot_hbm, slot),
        ("owner", owner_hbm, owner), ("q", q_hbm, q), ("lam", mul_hbm, lam), ("off", off_hbm, off),
        ("pre", pre_hbm, pre), ("inv", inv_hbm, inv),
    )):
        loads[name] = pltpu.make_async_copy(source, target, load_sem.at[number])
        loads[name].start()

    def plane_peer(offset):
        other = lax.rem(spot + offset, plane)
        return other, {"agents": high * fold + other // group, "group": lax.rem(other, group)}

    def line_peer(offset):
        return {"agents": lax.rem(high + offset, lines) * fold + low, "group": mine}

    def exists(step):
        return jnp.logical_and(me + step >= 0, me + step < agents)

    steps = [d for d in range(-SPAN, SPAN + 1) if d != 0]
    barrier = pltpu.get_barrier_semaphore()
    for offset in range(1, plane):
        pl.semaphore_signal(barrier, inc=1, device_id=plane_peer(offset)[1], device_id_type=MESH)
    for offset in range(1, lines):
        pl.semaphore_signal(barrier, inc=1, device_id=line_peer(offset), device_id_type=MESH)
    expected = plane - 1 + lines - 1
    for step in steps:
        @pl.when(exists(step))
        def _():
            pl.semaphore_signal(
                barrier, inc=1, device_id={"agents": me + step, "group": mine}, device_id_type=MESH
            )
        expected = expected + jnp.where(exists(step), 1, 0)

    def near_copy(turn, step):
        return pltpu.make_async_remote_copy(
            src_ref=traj.at[turn], dst_ref=near_in.at[turn, SPAN - step],
            send_sem=near_send.at[turn, SPAN + step], recv_sem=near_recv.at[turn, SPAN - step],
            device_id={"agents": me + step, "group": mine}, device_id_type=MESH)

    def near_arrival(turn, step):
        return pltpu.make_async_remote_copy(
            src_ref=traj.at[turn], dst_ref=near_in.at[turn, SPAN + step],
            send_sem=near_send.at[turn, SPAN + step], recv_sem=near_recv.at[turn, SPAN + step],
            device_id={"agents": me + step, "group": mine}, device_id_type=MESH)

    def rs_copy(turn, offset):
        other, device = plane_peer(offset)
        return pltpu.make_async_remote_copy(
            src_ref=rs_out.at[turn, other], dst_ref=rs_in.at[turn, offset],
            send_sem=rs_send.at[turn, offset], recv_sem=rs_recv.at[turn, offset],
            device_id=device, device_id_type=MESH)

    def line_copy(turn, offset):
        return pltpu.make_async_remote_copy(
            src_ref=line_out.at[turn], dst_ref=line_in.at[turn, offset],
            send_sem=line_send.at[turn, offset], recv_sem=line_recv.at[turn, offset],
            device_id=line_peer(offset), device_id_type=MESH)

    def ag_copy(turn, offset):
        return pltpu.make_async_remote_copy(
            src_ref=ag_out.at[turn], dst_ref=ag_in.at[turn, spot],
            send_sem=ag_send.at[turn, offset], recv_sem=ag_recv.at[turn, offset],
            device_id=plane_peer(offset)[1], device_id_type=MESH)

    def ag_arrival(turn, offset):
        return pltpu.make_async_remote_copy(
            src_ref=ag_out.at[turn], dst_ref=ag_in.at[turn, lax.rem(spot + plane - offset, plane)],
            send_sem=ag_send.at[turn, offset], recv_sem=ag_recv.at[turn, offset],
            device_id=plane_peer(offset)[1], device_id_type=MESH)

    def peak_copy(turn, offset):
        return pltpu.make_async_remote_copy(
            src_ref=peak_out.at[turn], dst_ref=peak_in.at[turn, offset],
            send_sem=peak_send.at[turn, offset], recv_sem=peak_recv.at[turn, offset],
            device_id=line_peer(offset), device_id_type=MESH)

    def top_copy(turn, offset):
        return pltpu.make_async_remote_copy(
            src_ref=top_out.at[turn], dst_ref=top_in.at[turn, offset],
            send_sem=top_send.at[turn, offset], recv_sem=top_recv.at[turn, offset],
            device_id=plane_peer(offset)[1], device_id_type=MESH)

    def onehot():
        names = lax.broadcasted_iota(jnp.int32, (NPLAT, block), 0)
        return jnp.where(names == plat[...], 1.0, 0.0).astype(BF16)

    def platoon_sums(value):
        hot = onehot()
        dims = (((1,), (1,)), ((), ()))
        first, second = split(value)
        return lax.dot_general(first, hot, dims, preferred_element_type=F32) + lax.dot_general(
            second, hot, dims, preferred_element_type=F32)

    def start_platoon(turn):
        sums = platoon_sums(traj[turn])
        for piece in range(plane):
            begin, end = min(rows, piece * part), min(rows, (piece + 1) * part)
            if end > begin:
                rs_out[turn, piece, 0:end - begin, :] = sums[begin:end, :]
            if turn == 0:
                ones = jnp.ones((16, block), BF16)
                if piece == 0:
                    counts = lax.dot_general(
                        ones, onehot(), (((1,), (1,)), ((), ())), preferred_element_type=F32)[0:1]
                rs_out[turn, piece, part:part + 1, :] = counts
        for offset in range(1, plane):
            rs_copy(turn, offset).start()

    def middle_platoon(turn):
        total = rs_out[turn, spot]
        for offset in range(1, plane):
            rs_copy(turn, offset).wait()
            total = total + rs_in[turn, offset]
        line_out[turn] = total
        for offset in range(1, lines):
            line_copy(turn, offset).start()

    def late_platoon(turn):
        total = line_out[turn]
        for offset in range(1, lines):
            line_copy(turn, offset).wait()
            total = total + line_in[turn, offset]
        if turn == 0:
            inv_count[...] = 1.0 / jnp.maximum(total[part:part + 1, :], 1.0)
        mean = total * inv_count[...]
        ag_out[turn] = mean
        for offset in range(1, plane):
            ag_copy(turn, offset).start()
        ag_in[turn, spot] = mean

    def finish_platoon(turn):
        for offset in range(1, plane):
            ag_copy(turn, offset).wait_send()
            ag_arrival(turn, offset).wait_recv()
        pieces = []
        for piece in range(plane):
            begin, end = min(rows, piece * part), min(rows, (piece + 1) * part)
            if end > begin:
                pieces.append(ag_in[turn, piece, 0:end - begin, :])
        means = jnp.concatenate(pieces, axis=0)
        hot = onehot()
        first, second = split(means)
        return jnp.dot(first, hot, preferred_element_type=F32) + jnp.dot(
            second, hot, preferred_element_type=F32)

    def start_near(turn):
        for step in steps:
            @pl.when(exists(step))
            def _():
                near_copy(turn, step).start()

    def wait_near(turn):
        for step in steps:
            @pl.when(exists(step))
            def _():
                near_copy(turn, step).wait_send()
                near_arrival(turn, step).wait_recv()

    def look(turn, slot_index, half):
        window = pl.ds(half * LANES, LANES)
        lane = lane_tab[slot_index, :, window]
        tile = tile_tab[slot_index, :, window]
        out = []
        for band in range(rows // 8):
            near = jnp.zeros((8, LANES), F32)
            for distance in range(2 * SPAN + 1):
                for side in range(halves):
                    span = (pl.ds(band * 8, 8), pl.ds(side * LANES, LANES))
                    if distance == SPAN:
                        source = traj[(turn,) + span]
                    else:
                        source = near_in[(turn, distance) + span]
                    taken = jnp.take_along_axis(source, lane, axis=1, mode="promise_in_bounds")
                    near = jnp.where(tile == distance * halves + side, taken, near)
            out.append(near)
        return tile >= 0, out

    def start_peak(turn, peak):
        peak_out[turn] = peak
        for offset in range(1, lines):
            peak_copy(turn, offset).start()

    def middle_peak(turn):
        peak = peak_out[turn]
        for offset in range(1, lines):
            peak_copy(turn, offset).wait()
            peak = jnp.maximum(peak, peak_in[turn, offset])
        top_out[turn] = peak
        for offset in range(1, plane):
            top_copy(turn, offset).start()

    def finish_peak(turn):
        peak = top_out[turn]
        for offset in range(1, plane):
            top_copy(turn, offset).wait()
            peak = jnp.maximum(peak, top_in[turn, offset])
        peak = jnp.max(jnp.max(peak, axis=0, keepdims=True), axis=1, keepdims=True)
        return 1.0 / (1.0 + peak)

    def tables():
        where = slot[...]
        tile = jnp.where(where >= 0, (owner[...] - me + SPAN) * halves + where // LANES, -1)
        lane = lax.rem(jnp.maximum(where, 0), LANES)
        for index in range(degree):
            lane_tab[index] = jnp.broadcast_to(lane[index:index + 1], (8, block))
            tile_tab[index] = jnp.broadcast_to(tile[index:index + 1], (8, block))

    def down(matrix, vector_ref, start):
        def body(band, total):
            rows8 = vector_ref[pl.ds(pl.multiple_of(band * 8, 8), 8), :]
            for index in range(8):
                total = total + matrix[band * 8 + index].astype(F32) * rows8[index:index + 1, :]
            return total
        return lax.fori_loop(0, rows // 8, body, start)

    loads["free"].wait()
    loads["plat"].wait()
    pl.semaphore_wait(barrier, expected)
    rs_out[...] = jnp.zeros_like(rs_out)
    start_platoon(0)
    start_near(0)
    for name in ("slot", "owner", "q", "lam", "off", "pre", "inv"):
        loads[name].wait()
    tables()
    middle_platoon(0)
    wait_near(0)
    late_platoon(0)

    coup[...] = jnp.zeros_like(coup)

    def first_body(index, carry):
        for half in range(halves):
            alive, near = look(0, index, half)
            for band in range(rows // 8):
                span = (pl.ds(band * 8, 8), pl.ds(half * LANES, LANES))
                term = lam[(index,) + span] - RHO * (near[band] + off[(index,) + span])
                coup[span] = coup[span] + jnp.where(alive, term, 0.0)
        return carry

    lax.fori_loop(0, degree, first_body, 0)

    for turn in range(ITERS):
        if turn > 0:
            factor = finish_peak(turn - 1)
            base = coup[...] + rhs[...] * factor
        else:
            base = coup[...]
        coup[...] = base - KAPPA * finish_platoon(turn)
        if turn > 0:
            lam[...] = lam[...] + gap[...] * factor[None]
        rhs[...] = down(pre, coup, q[...])
        plan[...] = -down(inv, rhs, jnp.zeros((rows, block), F32))
        current = plan[...]

        def up_body(band, carry):
            out = []
            for index in range(8):
                product = pre[band * 8 + index].astype(F32) * current
                out.append(jnp.sum(product, axis=0, keepdims=True))
            span = pl.ds(pl.multiple_of(band * 8, 8), 8)
            traj[turn + 1, span, :] = jnp.concatenate(out, axis=0) + traj[0, span, :]
            return carry

        lax.fori_loop(0, rows // 8, up_body, 0)
        more = turn + 1 < ITERS
        if more:
            start_platoon(turn + 1)
        start_near(turn + 1)
        if more:
            middle_platoon(turn + 1)
        wait_near(turn + 1)
        coup[...] = jnp.zeros_like(coup)
        rhs[...] = jnp.zeros_like(rhs)

        def body(index, peak):
            for half in range(halves):
                alive, near = look(turn + 1, index, half)
                for band in range(rows // 8):
                    span = (pl.ds(band * 8, 8), pl.ds(half * LANES, LANES))
                    wish = near[band] + off[(index,) + span]
                    miss = jnp.where(alive, traj[(turn + 1,) + span] - wish, 0.0)
                    gap[(index,) + span] = miss
                    peak = jnp.maximum(peak, jnp.abs(miss))
                    if more:
                        term = lam[(index,) + span] - RHO * wish
                        coup[span] = coup[span] + jnp.where(alive, term, 0.0)
                        rhs[span] = rhs[span] + miss
            return peak

        peak = lax.fori_loop(0, degree, body, jnp.zeros((8, LANES), F32))
        start_peak(turn, peak)
        if more:
            late_platoon(turn + 1)
        else:
            done_plan = pltpu.make_async_copy(plan, plan_hbm, store_sem.at[0])
            done_plan.start()
        middle_peak(turn)

    factor = finish_peak(ITERS - 1)
    lam[...] = lam[...] + gap[...] * factor[None]
    done_lam = pltpu.make_async_copy(lam, lam_hbm, store_sem.at[1])
    done_lam.start()
    done_plan.wait()
    done_lam.wait()


def local(agents, group, q_lin, inverse, predict, free_traj, offsets, multipliers, nbr_owner, nbr_slot, platoon):
    rows, block = q_lin.shape[1:]
    degree = nbr_slot.shape[1]
    fold = 2 if agents % 2 == 0 else 1
    lines, plane = agents // fold, fold * group
    part = -(-rows // plane)
    tile = (-(-(part + 1) // 8) * 8, NPLAT)
    turns = ITERS
    wide = 2 * SPAN + 1
    dma = lambda *shape: pltpu.SemaphoreType.DMA(shape)
    vmem = lambda *shape: pltpu.VMEM(shape, F32)
    anywhere = pl.BlockSpec(memory_space=pl.ANY)
    plan, lam = pl.pallas_call(
        functools.partial(kernel, agents, group, fold),
        out_shape=(
            jax.ShapeDtypeStruct((rows, block), F32),
            jax.ShapeDtypeStruct((degree, rows, block), F32),
        ),
        in_specs=[anywhere] * 9,
        out_specs=[anywhere] * 2,
        scratch_shapes=[
            vmem(rows, block),
            pltpu.VMEM((rows, rows, block), BF16),
            pltpu.VMEM((rows, rows, block), BF16),
            vmem(degree, rows, block),
            vmem(degree, rows, block),
            pltpu.VMEM((degree, block), jnp.int32),
            pltpu.VMEM((degree, block), jnp.int32),
            pltpu.VMEM((1, block), jnp.int32),
            vmem(rows, block),
            vmem(degree, rows, block),
            vmem(rows, block),
            vmem(rows, block),
            vmem(turns + 1, rows, block),
            vmem(turns + 1, wide, rows, block),
            vmem(turns, plane, *tile),
            vmem(turns, plane, *tile),
            vmem(turns, *tile),
            vmem(turns, lines, *tile),
            vmem(turns, *tile),
            vmem(turns, plane, *tile),
            vmem(turns, 8, LANES),
            vmem(turns, lines, 8, LANES),
            vmem(turns, 8, LANES),
            vmem(turns, plane, 8, LANES),
            vmem(1, NPLAT),
            pltpu.VMEM((degree, 8, block), jnp.int32),
            pltpu.VMEM((degree, 8, block), jnp.int32),
            dma(9), dma(2),
            dma(turns + 1, wide), dma(turns + 1, wide),
            dma(turns, plane), dma(turns, plane),
            dma(turns, lines), dma(turns, lines),
            dma(turns, plane), dma(turns, plane),
            dma(turns, lines), dma(turns, lines),
            dma(turns, plane), dma(turns, plane),
        ],
        compiler_params=pltpu.CompilerParams(collective_id=0, has_side_effects=True),
    )(
        q_lin[0], inverse[0], predict[0], free_traj[0], offsets[0], multipliers[0],
        nbr_owner[0], nbr_slot[0], platoon,
    )
    return plan[None], lam[None]


def solution(mesh):
    agents, group = mesh.shape["agents"], mesh.shape["group"]
    return jax.shard_map(
        functools.partial(local, agents, group),
        mesh=mesh,
        in_specs=(
            P("group", None, "agents"),
            P("group", None, None, "agents"),
            P("group", None, None, "agents"),
            P("group", None, "agents"),
            P("group", None, None, "agents"),
            P("group", None, None, "agents"),
            P("group", None, "agents"),
            P("group", None, "agents"),
            P("group", "agents"),
        ),
        out_specs=(P("group", None, "agents"), P("group", None, None, "agents")),
        check_vma=False,
    )
```

time: 355 us -> 62 us (0.17)
  blocking collectives: 244 us -> 0 us
  Pallas kernels: 0 us -> 58 us
  starting transfers between devices: 42.3 us -> 0 us
  local copies, waits for them, and re-layouts: 31.1 us -> 3.12 us
  other arithmetic: 16.1 us -> 0 us
  waiting for transfers between devices: 14 us -> 0 us
    psum x3 -> x0, blocking collectives: 124 us -> none  [the longest x2 80.8 us: local(): sums = lax.psum(platoon_local(traj), ('agents', 'group'))]
    pmax x3 -> x0, blocking collectives: 120 us -> none  [local(): peak = lax.pmax(local_peak, ('agents', 'group'))]
    pallas_call x0 -> x1, Pallas kernels: none -> 58 us  [local(): pl.pallas_call(functools.partial(kernel, agents, group, fold), out_shape=...]
    ppermute x16 -> x0, starting transfers between devices: 42.3 us -> none  [shifted(): lax.ppermute(value, axis, [(source, source + steps) for source in range(f...]
    gather x4 -> x0, local copies, waits for them, and re-layouts: 26.1 us -> none  [lookup(): jnp.take(joined[0], column, axis=1)]
    ppermute x16 -> x0, waiting for transfers between devices: 14 us -> none  [shifted(): lax.ppermute(value, axis, [(source, source + steps) for source in range(f...]
    reduce_sum x4 -> x0, other arithmetic: 4.35 us -> none  [the longest x3 3.57 us: local(): jnp.sum(live * (lam - RHO * (near + offsets)), axis=1) - KAPPA * attract]
    select_n x4 -> x0, other arithmetic: 3.79 us -> none  [lookup(): jnp.take(joined[0], column, axis=1)]
  transfers between devices with their start and end apart: 16 -> 0, of which waited for: 6 -> 0; matrix products, arithmetic and copies ran while one was open for 1% -> 0% of each run, Pallas kernels for 0% -> 0%
where the time goes in v1:
time: 62 us; the launch traced here: 61.8 us
  Pallas kernels  58 us (94%)
  local copies, waits for them, and re-layouts  3.12 us (5%)
  between operations  0.64 us (1%)
    pallas_call x1, Pallas kernels, local(): pl.pallas_call(functools.partial(kernel, agents, group, fold), out_shape=...  58 us
    unnamed x2, local copies, waits for them, and re-layouts  3.12 us

profile of v1, /device:TPU:0, one launch (start us, length us, event | category | flops | bytes accessed | tf_op | source)
XLA Modules:
  0.0 61.8 jit_solution(16940481539088639785)
XLA Ops:
  0.6 58.0 %shard_map.104 = (f32[40,256]{1,0:T(8,128)}, f32[8,40,256]{2,1,0:T(8,128)}) custom-call(f32[40,256]{1,0:T(8,128)} %bitcast.16, bf16[40,40,256]{2,1,0:T(8,128)(2,1)} %bitcast.10, bf16[40,40,256]{2,1,0:T(8,128)(2,1)} %bitcast.11, f32[40,256]{1,0:T(8,128)} %bitcast.17, f32[8,40,256]{2,1,0:T(8,128)} %bitcast.13, f32[8,40,256]{2,1,0:T(8,128)} %bitcast.14, ...), custom_call_target="tpu_custom_call" | custom-call | tf_op jit(solution)/shard_map/pallas_call | solution.py:369
  58.7 1.4 %copy.13 = f32[1,40,256]{2,1,0:T(8,128)} copy(f32[1,40,256]{2,1,0:T(8,128)} %bitcast.15) | data formatting | bytes 81920
  60.1 1.7 %copy.14 = f32[1,8,40,256]{3,2,1,0:T(8,128)} copy(f32[1,8,40,256]{3,2,1,0:T(8,128)} %bitcast.12) | data formatting | bytes 655360

commit v2 on v1

--- a/solution.py
+++ b/solution.py
@@ -15,6 +15,7 @@
 LANES = 128
 F32 = jnp.float32
 BF16 = jnp.bfloat16
+ORDER = 2
 MESH = pl.DeviceIdType.MESH
 
 
@@ -27,19 +28,20 @@
 def kernel(
     agents, group, fold,
     q_hbm, inv_hbm, pre_hbm, free_hbm, off_hbm, mul_hbm, owner_hbm, slot_hbm, plat_hbm,
-    plan_hbm, lam_hbm,
-    q, inv, pre, off, lam, owner, slot, plat,
-    plan, gap, coup, rhs, traj, near_in,
-    rs_out, rs_in, line_out, line_in, ag_out, ag_in, peak_out, peak_in, top_out, top_in,
+    plan, lam, gap, scale,
+    q, inv, pre, off, owner, slot, plat,
+    coup, rhs, miss_sum, slope, plan_slope, traj, near_in,
+    rs_out, rs_in, line_out, line_in, ag_out, ag_in, peak_out, peak_in,
     inv_count, lane_tab, tile_tab,
-    load_sem, store_sem,
+    load_sem,
     near_send, near_recv, rs_send, rs_recv, line_send, line_recv, ag_send, ag_recv,
-    peak_send, peak_recv, top_send, top_recv,
+    peak_send, peak_recv,
 ):
     me = lax.axis_index("agents")
     mine = lax.axis_index("group")
     lines = agents // fold
     plane = fold * group
+    everyone = agents * group
     high, low = me // fold, me % fold
     spot = low * group + mine
     rows, block = q.shape
@@ -119,16 +121,12 @@
             device_id=plane_peer(offset)[1], device_id_type=MESH)
 
     def peak_copy(turn, offset):
+        other = lax.rem(me * group + mine + offset, everyone)
         return pltpu.make_async_remote_copy(
             src_ref=peak_out.at[turn], dst_ref=peak_in.at[turn, offset],
-            send_sem=peak_send.at[turn, offset], recv_sem=peak_recv.at[turn, offset],
-            device_id=line_peer(offset), device_id_type=MESH)
-
-    def top_copy(turn, offset):
-        return pltpu.make_async_remote_copy(
-            src_ref=top_out.at[turn], dst_ref=top_in.at[turn, offset],
-            send_sem=top_send.at[turn, offset], recv_sem=top_recv.at[turn, offset],
-            device_id=plane_peer(offset)[1], device_id_type=MESH)
+            send_sem=peak_send.at[turn], recv_sem=peak_recv.at[turn],
+            device_id={"agents": other // group, "group": lax.rem(other, group)},
+            device_id_type=MESH)
 
     def onehot():
         names = lax.broadcasted_iota(jnp.int32, (NPLAT, block), 0)
@@ -193,7 +191,7 @@
         return jnp.dot(first, hot, preferred_element_type=F32) + jnp.dot(
             second, hot, preferred_element_type=F32)
 
-    def start_near(turn):
+    def start_near(turn, steps=steps):
         for step in steps:
             @pl.when(exists(step))
             def _():
@@ -226,26 +224,18 @@
         return tile >= 0, out
 
     def start_peak(turn, peak):
-        peak_out[turn] = peak
-        for offset in range(1, lines):
+        peak_out[turn] = jnp.max(peak, axis=0, keepdims=True)
+        for offset in range(1, everyone):
             peak_copy(turn, offset).start()
 
-    def middle_peak(turn):
+    def finish_peak(turn):
+        landed = peak_in.at[turn, pl.ds(1, everyone - 1)]
+        pltpu.make_async_copy(landed, landed, peak_send.at[turn]).wait()
+        pltpu.make_async_copy(landed, landed, peak_recv.at[turn]).wait()
         peak = peak_out[turn]
-        for offset in range(1, lines):
-            peak_copy(turn, offset).wait()
+        for offset in range(1, everyone):
             peak = jnp.maximum(peak, peak_in[turn, offset])
-        top_out[turn] = peak
-        for offset in range(1, plane):
-            top_copy(turn, offset).start()
-
-    def finish_peak(turn):
-        peak = top_out[turn]
-        for offset in range(1, plane):
-            top_copy(turn, offset).wait()
-            peak = jnp.maximum(peak, top_in[turn, offset])
-        peak = jnp.max(jnp.max(peak, axis=0, keepdims=True), axis=1, keepdims=True)
-        return 1.0 / (1.0 + peak)
+        return 1.0 / (1.0 + jnp.max(peak, axis=1, keepdims=True))
 
     def tables():
         where = slot[...]
@@ -289,38 +279,48 @@
 
     lax.fori_loop(0, degree, first_body, 0)
 
+    def up(vector, write):
+        def body(band, carry):
+            out = []
+            for index in range(8):
+                product = pre[band * 8 + index].astype(F32) * vector
+                out.append(jnp.sum(product, axis=0, keepdims=True))
+            write(pl.ds(pl.multiple_of(band * 8, 8), 8), jnp.concatenate(out, axis=0))
+            return carry
+
+        lax.fori_loop(0, rows // 8, body, 0)
+
+    empty = jnp.zeros((rows, block), F32)
     for turn in range(ITERS):
+        more = turn + 1 < ITERS
+        coup[...] = coup[...] - KAPPA * finish_platoon(turn)
+        rhs[...] = down(pre, coup, q[...])
+        plan[...] = -down(inv, rhs, empty)
+
+        def write_first(span, value):
+            traj[turn + 1, span, :] = value + traj[0, span, :]
+
+        up(plan[...], write_first)
         if turn > 0:
             factor = finish_peak(turn - 1)
-            base = coup[...] + rhs[...] * factor
-        else:
-            base = coup[...]
-        coup[...] = base - KAPPA * finish_platoon(turn)
-        if turn > 0:
-            lam[...] = lam[...] + gap[...] * factor[None]
-        rhs[...] = down(pre, coup, q[...])
-        plan[...] = -down(inv, rhs, jnp.zeros((rows, block), F32))
-        current = plan[...]
-
-        def up_body(band, carry):
-            out = []
-            for index in range(8):
-                product = pre[band * 8 + index].astype(F32) * current
-                out.append(jnp.sum(product, axis=0, keepdims=True))
-            span = pl.ds(pl.multiple_of(band * 8, 8), 8)
-            traj[turn + 1, span, :] = jnp.concatenate(out, axis=0) + traj[0, span, :]
-            return carry
-
-        lax.fori_loop(0, rows // 8, up_body, 0)
-        more = turn + 1 < ITERS
+            traj[turn + 1] = traj[turn + 1] + factor * slope[...]
+        if ORDER == 0:
+            start_near(turn + 1)
+        if ORDER == 2:
+            start_near(turn + 1, (-2, 2))
         if more:
             start_platoon(turn + 1)
-        start_near(turn + 1)
+        if ORDER == 1:
+            start_near(turn + 1)
+        if ORDER == 2:
+            start_near(turn + 1, (-1, 1))
+        if not more and turn > 0:
+            plan[...] = plan[...] + factor * plan_slope[...]
         if more:
             middle_platoon(turn + 1)
         wait_near(turn + 1)
         coup[...] = jnp.zeros_like(coup)
-        rhs[...] = jnp.zeros_like(rhs)
+        miss_sum[...] = jnp.zeros_like(miss_sum)
 
         def body(index, peak):
             for half in range(halves):
@@ -329,29 +329,42 @@
                     span = (pl.ds(band * 8, 8), pl.ds(half * LANES, LANES))
                     wish = near[band] + off[(index,) + span]
                     miss = jnp.where(alive, traj[(turn + 1,) + span] - wish, 0.0)
+                    held = lam[(index,) + span]
+                    if turn > 0:
+                        held = held + gap[(index,) + span] * factor
+                        lam[(index,) + span] = held
                     gap[(index,) + span] = miss
                     peak = jnp.maximum(peak, jnp.abs(miss))
                     if more:
-                        term = lam[(index,) + span] - RHO * wish
+                        term = held - RHO * wish
                         coup[span] = coup[span] + jnp.where(alive, term, 0.0)
-                        rhs[span] = rhs[span] + miss
+                        miss_sum[span] = miss_sum[span] + miss
             return peak
 
         peak = lax.fori_loop(0, degree, body, jnp.zeros((8, LANES), F32))
         start_peak(turn, peak)
         if more:
             late_platoon(turn + 1)
-        else:
-            done_plan = pltpu.make_async_copy(plan, plan_hbm, store_sem.at[0])
-            done_plan.start()
-        middle_peak(turn)
-
-    factor = finish_peak(ITERS - 1)
-    lam[...] = lam[...] + gap[...] * factor[None]
-    done_lam = pltpu.make_async_copy(lam, lam_hbm, store_sem.at[1])
-    done_lam.start()
-    done_plan.wait()
-    done_lam.wait()
+            rhs[...] = down(pre, miss_sum, empty)
+            plan_slope[...] = -down(inv, rhs, empty)
+
+            def write_slope(span, value):
+                slope[span, :] = value
+
+            up(plan_slope[...], write_slope)
+
+    scale[...] = jnp.broadcast_to(finish_peak(ITERS - 1), scale.shape)
+
+
+def finish(plan, lam, gap, scale, plan_hbm, lam_hbm, buffer, sems):
+    copies = [pltpu.make_async_copy(plan, plan_hbm, sems.at[0])]
+    copies[0].start()
+    for index in range(lam.shape[0]):
+        buffer[index] = lam[index] + gap[index] * scale[...]
+        copies.append(pltpu.make_async_copy(buffer.at[index], lam_hbm.at[index], sems.at[1 + index]))
+        copies[-1].start()
+    for copy in copies:
+        copy.wait()
 
 
 def local(agents, group, q_lin, inverse, predict, free_traj, offsets, multipliers, nbr_owner, nbr_slot, platoon):
@@ -366,25 +379,28 @@
     dma = lambda *shape: pltpu.SemaphoreType.DMA(shape)
     vmem = lambda *shape: pltpu.VMEM(shape, F32)
     anywhere = pl.BlockSpec(memory_space=pl.ANY)
-    plan, lam = pl.pallas_call(
+    whole = pl.BlockSpec(memory_space=pltpu.VMEM)
+    plan, lam, gap, scale = pl.pallas_call(
         functools.partial(kernel, agents, group, fold),
         out_shape=(
-            jax.ShapeDtypeStruct((rows, block), F32),
-            jax.ShapeDtypeStruct((degree, rows, block), F32),
+            pltpu.VMEM((rows, block), F32),
+            pltpu.VMEM((degree, rows, block), F32),
+            pltpu.VMEM((degree, rows, block), F32),
+            pltpu.VMEM((1, block), F32),
         ),
         in_specs=[anywhere] * 9,
-        out_specs=[anywhere] * 2,
+        out_specs=[whole] * 4,
         scratch_shapes=[
             vmem(rows, block),
             pltpu.VMEM((rows, rows, block), BF16),
             pltpu.VMEM((rows, rows, block), BF16),
-            vmem(degree, rows, block),
             vmem(degree, rows, block),
             pltpu.VMEM((degree, block), jnp.int32),
             pltpu.VMEM((degree, block), jnp.int32),
             pltpu.VMEM((1, block), jnp.int32),
             vmem(rows, block),
-            vmem(degree, rows, block),
+            vmem(rows, block),
+            vmem(rows, block),
             vmem(rows, block),
             vmem(rows, block),
             vmem(turns + 1, rows, block),
@@ -395,26 +411,33 @@
             vmem(turns, lines, *tile),
             vmem(turns, *tile),
             vmem(turns, plane, *tile),
-            vmem(turns, 8, LANES),
-            vmem(turns, lines, 8, LANES),
-            vmem(turns, 8, LANES),
-            vmem(turns, plane, 8, LANES),
+            vmem(turns, 1, LANES),
+            vmem(turns, agents * group, 1, LANES),
             vmem(1, NPLAT),
             pltpu.VMEM((degree, 8, block), jnp.int32),
             pltpu.VMEM((degree, 8, block), jnp.int32),
-            dma(9), dma(2),
+            dma(9),
             dma(turns + 1, wide), dma(turns + 1, wide),
             dma(turns, plane), dma(turns, plane),
             dma(turns, lines), dma(turns, lines),
             dma(turns, plane), dma(turns, plane),
-            dma(turns, lines), dma(turns, lines),
-            dma(turns, plane), dma(turns, plane),
+            dma(turns), dma(turns),
         ],
         compiler_params=pltpu.CompilerParams(collective_id=0, has_side_effects=True),
     )(
         q_lin[0], inverse[0], predict[0], free_traj[0], offsets[0], multipliers[0],
         nbr_owner[0], nbr_slot[0], platoon,
     )
+    plan, lam = pl.pallas_call(
+        finish,
+        out_shape=(
+            jax.ShapeDtypeStruct((rows, block), F32),
+            jax.ShapeDtypeStruct((degree, rows, block), F32),
+        ),
+        in_specs=[whole] * 4,
+        out_specs=[anywhere] * 2,
+        scratch_shapes=[vmem(degree, rows, block), dma(degree + 1)],
+    )(*(pltpu.with_memory_space_constraint(x, pltpu.VMEM) for x in (plan, lam, gap, scale)))
     return plan[None], lam[None]
 
 

time: 62 us -> 51.5 us (0.83)
  Pallas kernels: 58 us -> 50.7 us
  local copies, waits for them, and re-layouts: 3.12 us -> 0 us
    pallas_call x1, Pallas kernels: 58 us -> 49.9 us  [local(): pl.pallas_call(functools.partial(kernel, agents, group, fold), out_shape=...]
    unnamed x2 -> x0, local copies, waits for them, and re-layouts: 3.12 us -> none
    pallas_call x0 -> x1, Pallas kernels: none -> 0.81 us  [local(): pl.pallas_call(finish, out_shape=(jax.ShapeDtypeStruct((rows, block), F32...]
where the time goes in v2:
time: 51.5 us; the launch traced here: 51.3 us
  Pallas kernels  50.7 us (98%)
  between operations  0.64 us (1%)
    pallas_call x1, Pallas kernels, local(): pl.pallas_call(functools.partial(kernel, agents, group, fold), out_shape=...  49.9 us

profile of v2, /device:TPU:0, one launch (start us, length us, event | category | flops | bytes accessed | tf_op | source)
XLA Modules:
  0.0 51.3 jit_solution(17083064195405727092)
XLA Ops:
  0.6 49.9 %shard_map.104 = (f32[40,256]{1,0:T(8,128)S(1)}, f32[8,40,256]{2,1,0:T(8,128)S(1)}, f32[8,40,256]{2,1,0:T(8,128)S(1)}, f32[1,256]{1,0:T(1,128)S(1)}) custom-call(f32[40,256]{1,0:T(8,128)} %bitcast.14, bf16[40,40,256]{2,1,0:T(8,128)(2,1)} %bitcast.10, bf16[40,40,256]{2,1,0:T(8,128)(2,1)} %bitcast.11, f32[40,256]{1,0:T(8,128)} %bitcast.15, ...), custom_call_target="tpu_custom_call" | custom-call | tf_op jit(solution)/shard_map/pallas_call | solution.py:383
  50.5 0.8 %shard_map.105 = (f32[40,256]{1,0:T(8,128)}, f32[8,40,256]{2,1,0:T(8,128)}) custom-call(f32[40,256]{1,0:T(8,128)S(1)} %get-tuple-element.8.plan, f32[8,40,256]{2,1,0:T(8,128)S(1)} %get-tuple-element.9.lam, f32[8,40,256]{2,1,0:T(8,128)S(1)} %get-tuple-element.10.gap, f32[1,256]{1,0:T(1,128)S(1)} %get-tuple-element.11.scale), custom_call_target="tpu_custom_call" | custom-call | tf_op jit(solution)/shard_map/pallas_call | solution.py:431

commit v3 on v2

--- a/solution.py
+++ b/solution.py
@@ -139,7 +139,7 @@
         return lax.dot_general(first, hot, dims, preferred_element_type=F32) + lax.dot_general(
             second, hot, dims, preferred_element_type=F32)
 
-    def start_platoon(turn):
+    def store_sums(turn):
         sums = platoon_sums(traj[turn])
         for piece in range(plane):
             begin, end = min(rows, piece * part), min(rows, (piece + 1) * part)
@@ -151,8 +151,14 @@
                     counts = lax.dot_general(
                         ones, onehot(), (((1,), (1,)), ((), ())), preferred_element_type=F32)[0:1]
                 rs_out[turn, piece, part:part + 1, :] = counts
+
+    def send_sums(turn):
         for offset in range(1, plane):
             rs_copy(turn, offset).start()
+
+    def start_platoon(turn):
+        store_sums(turn)
+        send_sums(turn)
 
     def middle_platoon(turn):
         total = rs_out[turn, spot]
@@ -255,9 +261,10 @@
 
     loads["free"].wait()
     loads["plat"].wait()
+    rs_out[...] = jnp.zeros_like(rs_out)
+    store_sums(0)
     pl.semaphore_wait(barrier, expected)
-    rs_out[...] = jnp.zeros_like(rs_out)
-    start_platoon(0)
+    send_sums(0)
     start_near(0)
     for name in ("slot", "owner", "q", "lam", "off", "pre", "inv"):
         loads[name].wait()
@@ -370,10 +377,10 @@
 def local(agents, group, q_lin, inverse, predict, free_traj, offsets, multipliers, nbr_owner, nbr_slot, platoon):
     rows, block = q_lin.shape[1:]
     degree = nbr_slot.shape[1]
-    fold = 2 if agents % 2 == 0 else 1
+    fold = 1
     lines, plane = agents // fold, fold * group
     part = -(-rows // plane)
-    tile = (-(-(part + 1) // 8) * 8, NPLAT)
+    tile = (part + 1, NPLAT)
     turns = ITERS
     wide = 2 * SPAN + 1
     dma = lambda *shape: pltpu.SemaphoreType.DMA(shape)

time: 51.5 us -> 50.2 us (0.975)
  Pallas kernels: 50.7 us -> 49.4 us
    pallas_call x1, Pallas kernels: 49.9 us -> 48.6 us  [local(): pl.pallas_call(functools.partial(kernel, agents, group, fold), out_shape=...]
where the time goes in v3:
time: 50.2 us; the launch traced here: 50 us
  Pallas kernels  49.4 us (98%)
  between operations  0.64 us (1%)
    pallas_call x1, Pallas kernels, local(): pl.pallas_call(functools.partial(kernel, agents, group, fold), out_shape=...  48.6 us

profile of v3, /device:TPU:0, one launch (start us, length us, event | category | flops | bytes accessed | tf_op | source)
XLA Modules:
  0.0 50.0 jit_solution(5118437226054079975)
XLA Ops:
  0.6 48.6 %shard_map.104 = (f32[40,256]{1,0:T(8,128)S(1)}, f32[8,40,256]{2,1,0:T(8,128)S(1)}, f32[8,40,256]{2,1,0:T(8,128)S(1)}, f32[1,256]{1,0:T(1,128)S(1)}) custom-call(f32[40,256]{1,0:T(8,128)} %bitcast.14, bf16[40,40,256]{2,1,0:T(8,128)(2,1)} %bitcast.10, bf16[40,40,256]{2,1,0:T(8,128)(2,1)} %bitcast.11, f32[40,256]{1,0:T(8,128)} %bitcast.15, ...), custom_call_target="tpu_custom_call" | custom-call | tf_op jit(solution)/shard_map/pallas_call | solution.py:390
  49.2 0.8 %shard_map.105 = (f32[40,256]{1,0:T(8,128)}, f32[8,40,256]{2,1,0:T(8,128)}) custom-call(f32[40,256]{1,0:T(8,128)S(1)} %get-tuple-element.8.plan, f32[8,40,256]{2,1,0:T(8,128)S(1)} %get-tuple-element.9.lam, f32[8,40,256]{2,1,0:T(8,128)S(1)} %get-tuple-element.10.gap, f32[1,256]{1,0:T(1,128)S(1)} %get-tuple-element.11.scale), custom_call_target="tpu_custom_call" | custom-call | tf_op jit(solution)/shard_map/pallas_call | solution.py:438
